TPU v7x, 32 devices: a whole 2x2x4 slice. The times are simulated.
32 devices in a mesh: tm: 8 (over z, x), space: 4 (over y, core).
Axes of the slice: x: 2, y: 2, z: 4, core: 2. Of those that a mesh axis runs over, the one named last changes fastest.
Arguments:
- checkpoint: float32 [8, 4, 64, 1024], P('tm', None, 'space'), may hold values from -6 to 6
- advect: float32 [8, 2, 64, 1024], P('tm', None, 'space'), may hold values from -0.2 to 0.2
- diffuse: float32 [8, 64, 1024], P('tm', 'space'), may hold values from 0.1 to 0.2
- obs_rows: int32 [8, 8, 8], P('tm', None, 'space'), may hold values from 0 to 1
- obs_values: float32 [8, 8, 8, 4, 8, 1024], P('tm', None, 'space'), may hold values from -6 to 6
- obs_weight: float32 [8], P('tm'), may hold values from 0.5 to 13.5
- error_inverse: float32 [8, 4], P('tm'), may hold values from 0.3 to 3
- rates: float32 [8, 4], replicated, may hold values from 0.07924466 to 1, as said below
Outputs:
- direction: float32 [8, 4, 64, 1024], P('tm', None, 'space')
- grad_rms: float32 [], replicated
Inputs may be any that keep to these rules, and one draw needn't show every extreme that they name: `obs_rows`: entry i of the last dimension counts blocks of 8 rows within the rows of space block i // 2; repeats may occur. `rates`: every entry is below 1.
All inputs are finite; a program needn't handle non-finite values.
Results may differ from a plain program's by a relative error of at most 0.0003.
Values sent between devices are 32-bit elements; how exact they have to be, the bound alone decides.
A program may use at most 64 MiB of HBM per device.

v0:
```python
import jax
import jax.numpy as jnp
from jax import lax
from jax.sharding import PartitionSpec as P

STEPS = 8
BLOCK = 8


def padded_2(block, sides, width):
    for axis, dim in sides:
        count = lax.axis_size(axis)
        forward = [(i, i + 1) for i in range(count - 1)]
        backward = [(target, source) for source, target in forward]
        low = lax.ppermute(
            lax.slice_in_dim(block, block.shape[dim] - width, None, axis=dim), axis, forward
        )
        high = lax.ppermute(lax.slice_in_dim(block, 0, width, axis=dim), axis, backward)
        block = jnp.concatenate([low, block, high], axis=dim)
    return block


def passed_along(value, axis, steps):
    count = lax.axis_size(axis)
    leading, last = (max(0, -steps), min(count, count - steps))
    return lax.ppermute(value, axis, [(source, source + steps) for source in range(leading, last)])


def stencil_of(advect_one, diffuse_one):
    centre = 1.0 - 4.0 * diffuse_one
    to_east = diffuse_one - 0.5 * advect_one[0]
    to_west = diffuse_one + 0.5 * advect_one[0]
    to_north = diffuse_one - 0.5 * advect_one[1]
    to_south = diffuse_one + 0.5 * advect_one[1]
    return (centre, to_east, to_west, to_north, to_south)


def advance(field_now, stencil):
    centre, to_east, to_west, to_north, to_south = stencil
    padded = padded_2(field_now, (("space", 1),), 1)
    return (
        centre * field_now
        + to_east * jnp.roll(field_now, -1, axis=2)
        + to_west * jnp.roll(field_now, 1, axis=2)
        + to_north * padded[:, 2:]
        + to_south * padded[:, :-2]
    )


def retreat(costate, stencil, north_pad, south_pad):
    padded = padded_2(costate, (("space", 1),), 1)
    centre, to_east, to_west = (stencil[0], stencil[1], stencil[2])
    return (
        centre * costate
        + jnp.roll(to_east * costate, 1, axis=2)
        + jnp.roll(to_west * costate, -1, axis=2)
        + (north_pad * padded)[:, :-2]
        + (south_pad * padded)[:, 2:]
    )


def select_rows(field_now, picker):
    blocks = field_now.reshape(field_now.shape[0], picker.shape[1], BLOCK, field_now.shape[2])
    return jnp.einsum("kb,cbrx->kcrx", picker, blocks, precision=lax.Precision.HIGHEST)


def spread_rows(misfit, picker, field_shape):
    placed = jnp.einsum("kb,kcrx->cbrx", picker, misfit, precision=lax.Precision.HIGHEST)
    return placed.reshape(field_shape)


def weigh_own(field_now, initial, inverse_row):
    prior_end = passed_along(field_now, "tm", 1)
    return inverse_row[:, None, None] * (initial - prior_end)


def adjoint_sweep(misfits, pickers, weight, later_term, stencil, north_pad, south_pad, field_shape):
    costate = spread_rows(weight * misfits[STEPS - 1], pickers[STEPS - 1], field_shape) - later_term
    for moment in range(STEPS, 0, -1):
        costate = retreat(costate, stencil, north_pad, south_pad)
        if moment >= 2:
            costate = costate + spread_rows(
                weight * misfits[moment - 2], pickers[moment - 2], field_shape
            )
    return costate


def combine(earlier, latter):
    return (earlier[0] * latter[0], latter[0] * earlier[1] + latter[1])


def on_device(checkpoint, advect, diffuse, obs_rows, obs_values, obs_weight, error_inverse, rates):
    initial = checkpoint[0]
    field_shape = initial.shape
    stencil = stencil_of(advect[0], diffuse[0])
    rim_coefs = padded_2(jnp.stack([advect[0, 1], diffuse[0]]), (("space", 1),), 1)
    north_pad = rim_coefs[1] - 0.5 * rim_coefs[0]
    south_pad = rim_coefs[1] + 0.5 * rim_coefs[0]
    block_count = field_shape[1] // BLOCK
    block_ids = jnp.arange(block_count, dtype=jnp.int32)
    pickers = [
        (obs_rows[0, moment][:, None] == block_ids[None, :]).astype(jnp.float32)
        for moment in range(STEPS)
    ]
    field_now = initial
    misfits = []
    for moment in range(STEPS):
        field_now = advance(field_now, stencil)
        misfits.append(select_rows(field_now, pickers[moment]) - obs_values[0, moment])
    weight = obs_weight[0]
    weighted = weigh_own(field_now, initial, error_inverse[0])
    later_term = passed_along(weighted, "tm", -1)
    costate = adjoint_sweep(
        misfits, pickers, weight, later_term, stencil, north_pad, south_pad, field_shape
    )
    gradient = costate + weighted
    square_sum = lax.psum(jnp.sum(gradient * gradient), ("tm", "space"))
    entries = lax.axis_size("tm") * lax.axis_size("space") * gradient.size
    rms_value = jnp.sqrt(square_sum / entries + 1e-06)
    position = lax.axis_index("tm")
    windows = lax.axis_size("tm")
    innovation = jnp.sqrt(1.0 - rates * rates)
    next_rates = jnp.concatenate([rates[1:], jnp.zeros((1, rates.shape[1]), jnp.float32)], axis=0)
    column_count = gradient.size // windows
    flat_grad = gradient.reshape(1, gradient.size)
    columns = lax.all_to_all(flat_grad, "tm", split_axis=1, concat_axis=0, tiled=True)
    places = position * column_count + jnp.arange(column_count, dtype=jnp.int32)
    member = places // (field_shape[1] * field_shape[2])
    onehot = (member[None, :] == jnp.arange(field_shape[0], dtype=jnp.int32)[:, None]).astype(
        jnp.float32
    )
    rate_cols = jnp.dot(rates, onehot, precision=lax.Precision.HIGHEST)
    inno_cols = jnp.dot(innovation, onehot, precision=lax.Precision.HIGHEST)
    next_cols = jnp.dot(next_rates, onehot, precision=lax.Precision.HIGHEST)
    forward_cols = lax.associative_scan(combine, (rate_cols, inno_cols * columns), axis=0)[1]
    backward_cols = lax.associative_scan(
        combine, (next_cols, inno_cols * forward_cols), reverse=True, axis=0
    )[1]
    flat_back = lax.all_to_all(backward_cols, "tm", split_axis=0, concat_axis=1, tiled=True)
    smoothed = flat_back.reshape(field_shape)
    direction = (smoothed / rms_value)[None]
    return (direction, rms_value)


def solution(mesh):
    placed = (
        P("tm", None, "space", None),
        P("tm", None, "space", None),
        P("tm", "space", None),
        P("tm", None, "space"),
        P("tm", None, "space", None, None, None),
        P("tm"),
        P("tm", None),
        P(),
    )
    return jax.shard_map(
        on_device,
        mesh=mesh,
        in_specs=placed,
        out_specs=(P("tm", None, "space", None), P()),
        check_vma=False,
    )
```

profile of v0, /device:TPU:0, one launch (start us, length us, event | category | flops | bytes accessed | tf_op | source)
XLA Modules:
  0.0 239.0 jit_solution(10749359197541015536)
XLA Ops:
  1.6 2.4 %collective-permute-start.1 = (f32[4,1,1024]{2,1,0:T(1,128)S(1)}, f32[4,1,1024]{2,1,0:T(1,128)S(1)}, u32[]{:S(2)}, u32[]{:S(2)}) collective-permute-start(f32[4,1,1024]{2,1,0:T(1,128)S(1)} %get-tuple-element.99), channel_id=1, source_target_pairs={{0,1},{1,2},{2,3},{4,5},{5,6},{6,7},{8,9},{9,10},{10,11},{12,13},{... | collective-permute-start | bytes 49160 | tf_op jit(solution)/shard_map/ppermute | solution.py:15
  8.3 5.8 %collective-permute-start.18 = (f32[2,1,1024]{2,1,0:T(1,128)S(1)}, f32[2,1,1024]{2,1,0:T(1,128)S(1)}, u32[]{:S(2)}, u32[]{:S(2)}) collective-permute-start(f32[2,1,1024]{2,1,0:T(1,128)S(1)} %get-tuple-element.114), channel_id=1, source_target_pairs={{0,1},{1,2},{2,3},{4,5},{5,6},{6,7},{8,9},{9,10},{10,11},{12,13},{... | collective-permute-start | bytes 24584 | tf_op jit(solution)/shard_map/ppermute | solution.py:15
  17.1 1.7 fusion.161
  20.3 3.6 %collective-permute-start.3 = (f32[4,1,1024]{2,1,0:T(1,128)S(1)}, f32[4,1,1024]{2,1,0:T(1,128)S(1)}, u32[]{:S(2)}, u32[]{:S(2)}) collective-permute-start(f32[4,1,1024]{2,1,0:T(1,128)S(1)} %get-tuple-element.93), channel_id=1, source_target_pairs={{0,1},{1,2},{2,3},{4,5},{5,6},{6,7},{8,9},{9,10},{10,11},{12,13},{... | collective-permute-start | bytes 49160 | tf_op jit(solution)/shard_map/ppermute | solution.py:15
  27.4 4.4 %collective-permute-start.5 = (f32[4,1,1024]{2,1,0:T(1,128)S(1)}, f32[4,1,1024]{2,1,0:T(1,128)S(1)}, u32[]{:S(2)}, u32[]{:S(2)}) collective-permute-start(f32[4,1,1024]{2,1,0:T(1,128)S(1)} %get-tuple-element.87), channel_id=1, source_target_pairs={{0,1},{1,2},{2,3},{4,5},{5,6},{6,7},{8,9},{9,10},{10,11},{12,13},{... | collective-permute-start | bytes 49160 | tf_op jit(solution)/shard_map/ppermute | solution.py:15
  35.2 4.2 %collective-permute-start.7 = (f32[4,1,1024]{2,1,0:T(1,128)S(1)}, f32[4,1,1024]{2,1,0:T(1,128)S(1)}, u32[]{:S(2)}, u32[]{:S(2)}) collective-permute-start(f32[4,1,1024]{2,1,0:T(1,128)S(1)} %get-tuple-element.81), channel_id=1, source_target_pairs={{0,1},{1,2},{2,3},{4,5},{5,6},{6,7},{8,9},{9,10},{10,11},{12,13},{... | collective-permute-start | bytes 49160 | tf_op jit(solution)/shard_map/ppermute | solution.py:15
  42.8 4.2 %collective-permute-start.9 = (f32[4,1,1024]{2,1,0:T(1,128)S(1)}, f32[4,1,1024]{2,1,0:T(1,128)S(1)}, u32[]{:S(2)}, u32[]{:S(2)}) collective-permute-start(f32[4,1,1024]{2,1,0:T(1,128)S(1)} %get-tuple-element.75), channel_id=1, source_target_pairs={{0,1},{1,2},{2,3},{4,5},{5,6},{6,7},{8,9},{9,10},{10,11},{12,13},{... | collective-permute-start | bytes 49160 | tf_op jit(solution)/shard_map/ppermute | solution.py:15
  50.4 4.2 %collective-permute-start.11 = (f32[4,1,1024]{2,1,0:T(1,128)S(1)}, f32[4,1,1024]{2,1,0:T(1,128)S(1)}, u32[]{:S(2)}, u32[]{:S(2)}) collective-permute-start(f32[4,1,1024]{2,1,0:T(1,128)S(1)} %get-tuple-element.69), channel_id=1, source_target_pairs={{0,1},{1,2},{2,3},{4,5},{5,6},{6,7},{8,9},{9,10},{10,11},{12,13},{... | collective-permute-start | bytes 49160 | tf_op jit(solution)/shard_map/ppermute | solution.py:15
  57.9 4.2 %collective-permute-start.13 = (f32[4,1,1024]{2,1,0:T(1,128)S(1)}, f32[4,1,1024]{2,1,0:T(1,128)S(1)}, u32[]{:S(2)}, u32[]{:S(2)}) collective-permute-start(f32[4,1,1024]{2,1,0:T(1,128)S(1)} %get-tuple-element.63), channel_id=1, source_target_pairs={{0,1},{1,2},{2,3},{4,5},{5,6},{6,7},{8,9},{9,10},{10,11},{12,13},{... | collective-permute-start | bytes 49160 | tf_op jit(solution)/shard_map/ppermute | solution.py:15
  62.1 1.5 collective-permute-start.12
  65.6 4.1 %collective-permute-start.15 = (f32[4,1,1024]{2,1,0:T(1,128)S(1)}, f32[4,1,1024]{2,1,0:T(1,128)S(1)}, u32[]{:S(2)}, u32[]{:S(2)}) collective-permute-start(f32[4,1,1024]{2,1,0:T(1,128)S(1)} %get-tuple-element.57), channel_id=1, source_target_pairs={{0,1},{1,2},{2,3},{4,5},{5,6},{6,7},{8,9},{9,10},{10,11},{12,13},{... | collective-permute-start | bytes 49160 | tf_op jit(solution)/shard_map/ppermute | solution.py:15
  71.1 1.7 collective-permute-done.14
  73.0 3.4 %collective-permute-start.16 = (f32[4,16,1024]{2,1,0:T(8,128)S(1)}, f32[4,16,1024]{2,1,0:T(8,128)S(1)}, u32[]{:S(2)}, u32[]{:S(2)}) collective-permute-start(f32[4,16,1024]{2,1,0:T(8,128)S(1)} %fusion.33), channel_id=1, source_target_pairs={{0,4},{4,8},{8,12},{12,16},{16,20},{20,24},{24,28},{1,5},{5,9},{9,... | collective-permute-start | bytes 786440 | tf_op jit(solution)/shard_map/ppermute | solution.py:26
  78.0 3.6 %collective-permute-done.16 = f32[4,16,1024]{2,1,0:T(8,128)S(1)} collective-permute-done((f32[4,16,1024]{2,1,0:T(8,128)S(1)}, f32[4,16,1024]{2,1,0:T(8,128)S(1)}, u32[]{:S(2)}, u32[]{:S(2)}) %collective-permute-start.16) | collective-permute-done | bytes 262176 | tf_op jit(solution)/shard_map/ppermute | solution.py:26
  84.6 8.1 %collective-permute-done.17 = f32[4,16,1024]{2,1,0:T(8,128)S(1)} collective-permute-done((f32[4,16,1024]{2,1,0:T(8,128)S(1)}, f32[4,16,1024]{2,1,0:T(8,128)S(1)}, u32[]{:S(2)}, u32[]{:S(2)}) %collective-permute-start.17) | collective-permute-done | bytes 262176 | tf_op jit(solution)/shard_map/ppermute | solution.py:26
  94.1 3.0 %collective-permute-start.20 = (f32[4,1,1024]{2,1,0:T(1,128)S(1)}, f32[4,1,1024]{2,1,0:T(1,128)S(1)}, u32[]{:S(2)}, u32[]{:S(2)}) collective-permute-start(f32[4,1,1024]{2,1,0:T(1,128)S(1)} %get-tuple-element.50), channel_id=1, source_target_pairs={{0,1},{1,2},{2,3},{4,5},{5,6},{6,7},{8,9},{9,10},{10,11},{12,13},{... | collective-permute-start | bytes 49160 | tf_op jit(solution)/shard_map/ppermute | solution.py:15
  99.6 4.2 %collective-permute-start.22 = (f32[4,1,1024]{2,1,0:T(1,128)S(1)}, f32[4,1,1024]{2,1,0:T(1,128)S(1)}, u32[]{:S(2)}, u32[]{:S(2)}) collective-permute-start(f32[4,1,1024]{2,1,0:T(1,128)S(1)} %get-tuple-element.48), channel_id=1, source_target_pairs={{0,1},{1,2},{2,3},{4,5},{5,6},{6,7},{8,9},{9,10},{10,11},{12,13},{... | collective-permute-start | bytes 49160 | tf_op jit(solution)/shard_map/ppermute | solution.py:15
  106.3 4.9 %collective-permute-start.24 = (f32[4,1,1024]{2,1,0:T(1,128)S(1)}, f32[4,1,1024]{2,1,0:T(1,128)S(1)}, u32[]{:S(2)}, u32[]{:S(2)}) collective-permute-start(f32[4,1,1024]{2,1,0:T(1,128)S(1)} %get-tuple-element.46), channel_id=1, source_target_pairs={{0,1},{1,2},{2,3},{4,5},{5,6},{6,7},{8,9},{9,10},{10,11},{12,13},{... | collective-permute-start | bytes 49160 | tf_op jit(solution)/shard_map/ppermute | solution.py:15
  113.6 4.9 %collective-permute-start.26 = (f32[4,1,1024]{2,1,0:T(1,128)S(1)}, f32[4,1,1024]{2,1,0:T(1,128)S(1)}, u32[]{:S(2)}, u32[]{:S(2)}) collective-permute-start(f32[4,1,1024]{2,1,0:T(1,128)S(1)} %get-tuple-element.44), channel_id=1, source_target_pairs={{0,1},{1,2},{2,3},{4,5},{5,6},{6,7},{8,9},{9,10},{10,11},{12,13},{... | collective-permute-start | bytes 49160 | tf_op jit(solution)/shard_map/ppermute | solution.py:15
  120.9 4.9 %collective-permute-start.28 = (f32[4,1,1024]{2,1,0:T(1,128)S(1)}, f32[4,1,1024]{2,1,0:T(1,128)S(1)}, u32[]{:S(2)}, u32[]{:S(2)}) collective-permute-start(f32[4,1,1024]{2,1,0:T(1,128)S(1)} %get-tuple-element.42), channel_id=1, source_target_pairs={{0,1},{1,2},{2,3},{4,5},{5,6},{6,7},{8,9},{9,10},{10,11},{12,13},{... | collective-permute-start | bytes 49160 | tf_op jit(solution)/shard_map/ppermute | solution.py:15
  128.3 4.9 %collective-permute-start.30 = (f32[4,1,1024]{2,1,0:T(1,128)S(1)}, f32[4,1,1024]{2,1,0:T(1,128)S(1)}, u32[]{:S(2)}, u32[]{:S(2)}) collective-permute-start(f32[4,1,1024]{2,1,0:T(1,128)S(1)} %get-tuple-element.40), channel_id=1, source_target_pairs={{0,1},{1,2},{2,3},{4,5},{5,6},{6,7},{8,9},{9,10},{10,11},{12,13},{... | collective-permute-start | bytes 49160 | tf_op jit(solution)/shard_map/ppermute | solution.py:15
  135.6 4.9 %collective-permute-start.32 = (f32[4,1,1024]{2,1,0:T(1,128)S(1)}, f32[4,1,1024]{2,1,0:T(1,128)S(1)}, u32[]{:S(2)}, u32[]{:S(2)}) collective-permute-start(f32[4,1,1024]{2,1,0:T(1,128)S(1)} %get-tuple-element.38), channel_id=1, source_target_pairs={{0,1},{1,2},{2,3},{4,5},{5,6},{6,7},{8,9},{9,10},{10,11},{12,13},{... | collective-permute-start | bytes 49160 | tf_op jit(solution)/shard_map/ppermute | solution.py:15
  142.9 4.9 %collective-permute-start.34 = (f32[4,1,1024]{2,1,0:T(1,128)S(1)}, f32[4,1,1024]{2,1,0:T(1,128)S(1)}, u32[]{:S(2)}, u32[]{:S(2)}) collective-permute-start(f32[4,1,1024]{2,1,0:T(1,128)S(1)} %get-tuple-element.36), channel_id=1, source_target_pairs={{0,1},{1,2},{2,3},{4,5},{5,6},{6,7},{8,9},{9,10},{10,11},{12,13},{... | collective-permute-start | bytes 49160 | tf_op jit(solution)/shard_map/ppermute | solution.py:15
  150.5 6.3 %all-to-all-start = ((f32[1,8,8192]{2,0,1:T(1,128)}), f32[1,8,8192]{2,0,1:T(1,128)S(1)}, u32[]{:S(2)}, u32[]{:S(2)}) async-start(f32[1,8,8192]{2,0,1:T(1,128)} %all_to_all.27), calls=%async_computation | async-start | bytes 524288 | tf_op jit(solution)/shard_map/all_to_all | solution.py:126
  162.4 1.6 slice.797
  164.0 1.6 slice.806
  165.5 1.6 slice.799
  175.8 1.6 slice.803
  177.4 1.6 slice.801
  181.7 1.6 slice.819
  185.9 6.0 %all-to-all-start.1 = ((f32[8,1,8192]{2,1,0:T(1,128)}), f32[8,1,8192]{2,1,0:T(1,128)S(1)}, u32[]{:S(2)}, u32[]{:S(2)}) async-start(f32[8,1,8192]{2,1,0:T(1,128)} %copy.67), calls=%async_computation.1 | async-start | bytes 524288 | tf_op jit(solution)/shard_map/all_to_all | solution.py:139
  191.9 43.9 %psum.7 = f32[]{:T(128)} all-reduce(f32[]{:T(128)} %get-tuple-element.10), channel_id=1, replica_groups=mesh['tm'=8,'space'=4] {'tm','space'}, use_global_device_ids=true, to_apply=%region_1.2 | all-reduce | flops 1 | bytes 8 | tf_op jit(solution)/shard_map/psum | solution.py:117
  (236 shorter events, 75.6 us)
Async XLA Ops:
  1.6 18.3 %collective-permute-start.1 = (f32[4,1,1024]{2,1,0:T(1,128)S(1)}, f32[4,1,1024]{2,1,0:T(1,128)S(1)}, u32[]{:S(2)}, u32[]{:S(2)}) collective-permute-start(f32[4,1,1024]{2,1,0:T(1,128)S(1)} %get-tuple-element.99), channel_id=1, source_target_pairs={{0,1},{1,2},{2,3},{4,5},{5,6},{6,7},{8,9},{9,10},{10,11},{12,13},{... | collective-permute-start | bytes 49160 | tf_op jit(solution)/shard_map/ppermute | solution.py:15
  4.0 15.9 %collective-permute-start = (f32[4,1,1024]{2,1,0:T(1,128)S(1)}, f32[4,1,1024]{2,1,0:T(1,128)S(1)}, u32[]{:S(2)}, u32[]{:S(2)}) collective-permute-start(f32[4,1,1024]{2,1,0:T(1,128)S(1)} %get-tuple-element.98), channel_id=1, source_target_pairs={{1,0},{2,1},{3,2},{5,4},{6,5},{7,6},{9,8},{10,9},{11,10},{13,12},{... | collective-permute-start | bytes 49160 | tf_op jit(solution)/shard_map/ppermute | solution.py:18
  7.0 12.8 %collective-permute-start.19 = (f32[2,1,1024]{2,1,0:T(1,128)S(1)}, f32[2,1,1024]{2,1,0:T(1,128)S(1)}, u32[]{:S(2)}, u32[]{:S(2)}) collective-permute-start(f32[2,1,1024]{2,1,0:T(1,128)S(1)} %get-tuple-element.115), channel_id=1, source_target_pairs={{1,0},{2,1},{3,2},{5,4},{6,5},{7,6},{9,8},{10,9},{11,10},{13,12},{... | collective-permute-start | bytes 24584 | tf_op jit(solution)/shard_map/ppermute | solution.py:18
  8.3 11.5 %collective-permute-start.18 = (f32[2,1,1024]{2,1,0:T(1,128)S(1)}, f32[2,1,1024]{2,1,0:T(1,128)S(1)}, u32[]{:S(2)}, u32[]{:S(2)}) collective-permute-start(f32[2,1,1024]{2,1,0:T(1,128)S(1)} %get-tuple-element.114), channel_id=1, source_target_pairs={{0,1},{1,2},{2,3},{4,5},{5,6},{6,7},{8,9},{9,10},{10,11},{12,13},{... | collective-permute-start | bytes 24584 | tf_op jit(solution)/shard_map/ppermute | solution.py:15
  20.3 6.6 %collective-permute-start.3 = (f32[4,1,1024]{2,1,0:T(1,128)S(1)}, f32[4,1,1024]{2,1,0:T(1,128)S(1)}, u32[]{:S(2)}, u32[]{:S(2)}) collective-permute-start(f32[4,1,1024]{2,1,0:T(1,128)S(1)} %get-tuple-element.93), channel_id=1, source_target_pairs={{0,1},{1,2},{2,3},{4,5},{5,6},{6,7},{8,9},{9,10},{10,11},{12,13},{... | collective-permute-start | bytes 49160 | tf_op jit(solution)/shard_map/ppermute | solution.py:15
  27.4 7.3 %collective-permute-start.5 = (f32[4,1,1024]{2,1,0:T(1,128)S(1)}, f32[4,1,1024]{2,1,0:T(1,128)S(1)}, u32[]{:S(2)}, u32[]{:S(2)}) collective-permute-start(f32[4,1,1024]{2,1,0:T(1,128)S(1)} %get-tuple-element.87), channel_id=1, source_target_pairs={{0,1},{1,2},{2,3},{4,5},{5,6},{6,7},{8,9},{9,10},{10,11},{12,13},{... | collective-permute-start | bytes 49160 | tf_op jit(solution)/shard_map/ppermute | solution.py:15
  35.2 7.1 %collective-permute-start.7 = (f32[4,1,1024]{2,1,0:T(1,128)S(1)}, f32[4,1,1024]{2,1,0:T(1,128)S(1)}, u32[]{:S(2)}, u32[]{:S(2)}) collective-permute-start(f32[4,1,1024]{2,1,0:T(1,128)S(1)} %get-tuple-element.81), channel_id=1, source_target_pairs={{0,1},{1,2},{2,3},{4,5},{5,6},{6,7},{8,9},{9,10},{10,11},{12,13},{... | collective-permute-start | bytes 49160 | tf_op jit(solution)/shard_map/ppermute | solution.py:15
  42.8 7.1 %collective-permute-start.9 = (f32[4,1,1024]{2,1,0:T(1,128)S(1)}, f32[4,1,1024]{2,1,0:T(1,128)S(1)}, u32[]{:S(2)}, u32[]{:S(2)}) collective-permute-start(f32[4,1,1024]{2,1,0:T(1,128)S(1)} %get-tuple-element.75), channel_id=1, source_target_pairs={{0,1},{1,2},{2,3},{4,5},{5,6},{6,7},{8,9},{9,10},{10,11},{12,13},{... | collective-permute-start | bytes 49160 | tf_op jit(solution)/shard_map/ppermute | solution.py:15
  50.4 7.1 %collective-permute-start.11 = (f32[4,1,1024]{2,1,0:T(1,128)S(1)}, f32[4,1,1024]{2,1,0:T(1,128)S(1)}, u32[]{:S(2)}, u32[]{:S(2)}) collective-permute-start(f32[4,1,1024]{2,1,0:T(1,128)S(1)} %get-tuple-element.69), channel_id=1, source_target_pairs={{0,1},{1,2},{2,3},{4,5},{5,6},{6,7},{8,9},{9,10},{10,11},{12,13},{... | collective-permute-start | bytes 49160 | tf_op jit(solution)/shard_map/ppermute | solution.py:15
  57.9 7.3 %collective-permute-start.13 = (f32[4,1,1024]{2,1,0:T(1,128)S(1)}, f32[4,1,1024]{2,1,0:T(1,128)S(1)}, u32[]{:S(2)}, u32[]{:S(2)}) collective-permute-start(f32[4,1,1024]{2,1,0:T(1,128)S(1)} %get-tuple-element.63), channel_id=1, source_target_pairs={{0,1},{1,2},{2,3},{4,5},{5,6},{6,7},{8,9},{9,10},{10,11},{12,13},{... | collective-permute-start | bytes 49160 | tf_op jit(solution)/shard_map/ppermute | solution.py:15
  62.1 3.1 %collective-permute-start.12 = (f32[4,1,1024]{2,1,0:T(1,128)S(1)}, f32[4,1,1024]{2,1,0:T(1,128)S(1)}, u32[]{:S(2)}, u32[]{:S(2)}) collective-permute-start(f32[4,1,1024]{2,1,0:T(1,128)S(1)} %get-tuple-element.62), channel_id=1, source_target_pairs={{1,0},{2,1},{3,2},{5,4},{6,5},{7,6},{9,8},{10,9},{11,10},{13,12},{... | collective-permute-start | bytes 49160 | tf_op jit(solution)/shard_map/ppermute | solution.py:18
  65.6 5.5 %collective-permute-start.15 = (f32[4,1,1024]{2,1,0:T(1,128)S(1)}, f32[4,1,1024]{2,1,0:T(1,128)S(1)}, u32[]{:S(2)}, u32[]{:S(2)}) collective-permute-start(f32[4,1,1024]{2,1,0:T(1,128)S(1)} %get-tuple-element.57), channel_id=1, source_target_pairs={{0,1},{1,2},{2,3},{4,5},{5,6},{6,7},{8,9},{9,10},{10,11},{12,13},{... | collective-permute-start | bytes 49160 | tf_op jit(solution)/shard_map/ppermute | solution.py:15
  73.0 8.6 %collective-permute-start.16 = (f32[4,16,1024]{2,1,0:T(8,128)S(1)}, f32[4,16,1024]{2,1,0:T(8,128)S(1)}, u32[]{:S(2)}, u32[]{:S(2)}) collective-permute-start(f32[4,16,1024]{2,1,0:T(8,128)S(1)} %fusion.33), channel_id=1, source_target_pairs={{0,4},{4,8},{8,12},{12,16},{16,20},{20,24},{24,28},{1,5},{5,9},{9,... | collective-permute-start | bytes 786440 | tf_op jit(solution)/shard_map/ppermute | solution.py:26
  81.7 10.9 %collective-permute-start.17 = (f32[4,16,1024]{2,1,0:T(8,128)S(1)}, f32[4,16,1024]{2,1,0:T(8,128)S(1)}, u32[]{:S(2)}, u32[]{:S(2)}) collective-permute-start(f32[4,16,1024]{2,1,0:T(8,128)S(1)} %subtract_multiply_fusion), channel_id=1, source_target_pairs={{4,0},{8,4},{12,8},{16,12},{20,16},{24,20},{28,24},{5,1},{9,5},{13... | collective-permute-start | bytes 786440 | tf_op jit(solution)/shard_map/ppermute | solution.py:26
  92.8 4.6 %collective-permute-start.21 = (f32[4,1,1024]{2,1,0:T(1,128)S(1)}, f32[4,1,1024]{2,1,0:T(1,128)S(1)}, u32[]{:S(2)}, u32[]{:S(2)}) collective-permute-start(f32[4,1,1024]{2,1,0:T(1,128)S(1)} %get-tuple-element.51), channel_id=1, source_target_pairs={{1,0},{2,1},{3,2},{5,4},{6,5},{7,6},{9,8},{10,9},{11,10},{13,12},{... | collective-permute-start | bytes 49160 | tf_op jit(solution)/shard_map/ppermute | solution.py:18
  94.1 3.9 %collective-permute-start.20 = (f32[4,1,1024]{2,1,0:T(1,128)S(1)}, f32[4,1,1024]{2,1,0:T(1,128)S(1)}, u32[]{:S(2)}, u32[]{:S(2)}) collective-permute-start(f32[4,1,1024]{2,1,0:T(1,128)S(1)} %get-tuple-element.50), channel_id=1, source_target_pairs={{0,1},{1,2},{2,3},{4,5},{5,6},{6,7},{8,9},{9,10},{10,11},{12,13},{... | collective-permute-start | bytes 49160 | tf_op jit(solution)/shard_map/ppermute | solution.py:15
  98.3 5.8 %collective-permute-start.23 = (f32[4,1,1024]{2,1,0:T(1,128)S(1)}, f32[4,1,1024]{2,1,0:T(1,128)S(1)}, u32[]{:S(2)}, u32[]{:S(2)}) collective-permute-start(f32[4,1,1024]{2,1,0:T(1,128)S(1)} %get-tuple-element.49), channel_id=1, source_target_pairs={{1,0},{2,1},{3,2},{5,4},{6,5},{7,6},{9,8},{10,9},{11,10},{13,12},{... | collective-permute-start | bytes 49160 | tf_op jit(solution)/shard_map/ppermute | solution.py:18
  99.6 5.0 %collective-permute-start.22 = (f32[4,1,1024]{2,1,0:T(1,128)S(1)}, f32[4,1,1024]{2,1,0:T(1,128)S(1)}, u32[]{:S(2)}, u32[]{:S(2)}) collective-permute-start(f32[4,1,1024]{2,1,0:T(1,128)S(1)} %get-tuple-element.48), channel_id=1, source_target_pairs={{0,1},{1,2},{2,3},{4,5},{5,6},{6,7},{8,9},{9,10},{10,11},{12,13},{... | collective-permute-start | bytes 49160 | tf_op jit(solution)/shard_map/ppermute | solution.py:15
  105.0 6.4 %collective-permute-start.25 = (f32[4,1,1024]{2,1,0:T(1,128)S(1)}, f32[4,1,1024]{2,1,0:T(1,128)S(1)}, u32[]{:S(2)}, u32[]{:S(2)}) collective-permute-start(f32[4,1,1024]{2,1,0:T(1,128)S(1)} %get-tuple-element.47), channel_id=1, source_target_pairs={{1,0},{2,1},{3,2},{5,4},{6,5},{7,6},{9,8},{10,9},{11,10},{13,12},{... | collective-permute-start | bytes 49160 | tf_op jit(solution)/shard_map/ppermute | solution.py:18
  106.3 5.7 %collective-permute-start.24 = (f32[4,1,1024]{2,1,0:T(1,128)S(1)}, f32[4,1,1024]{2,1,0:T(1,128)S(1)}, u32[]{:S(2)}, u32[]{:S(2)}) collective-permute-start(f32[4,1,1024]{2,1,0:T(1,128)S(1)} %get-tuple-element.46), channel_id=1, source_target_pairs={{0,1},{1,2},{2,3},{4,5},{5,6},{6,7},{8,9},{9,10},{10,11},{12,13},{... | collective-permute-start | bytes 49160 | tf_op jit(solution)/shard_map/ppermute | solution.py:15
  112.3 6.4 %collective-permute-start.27 = (f32[4,1,1024]{2,1,0:T(1,128)S(1)}, f32[4,1,1024]{2,1,0:T(1,128)S(1)}, u32[]{:S(2)}, u32[]{:S(2)}) collective-permute-start(f32[4,1,1024]{2,1,0:T(1,128)S(1)} %get-tuple-element.45), channel_id=1, source_target_pairs={{1,0},{2,1},{3,2},{5,4},{6,5},{7,6},{9,8},{10,9},{11,10},{13,12},{... | collective-permute-start | bytes 49160 | tf_op jit(solution)/shard_map/ppermute | solution.py:18
  113.6 5.7 %collective-permute-start.26 = (f32[4,1,1024]{2,1,0:T(1,128)S(1)}, f32[4,1,1024]{2,1,0:T(1,128)S(1)}, u32[]{:S(2)}, u32[]{:S(2)}) collective-permute-start(f32[4,1,1024]{2,1,0:T(1,128)S(1)} %get-tuple-element.44), channel_id=1, source_target_pairs={{0,1},{1,2},{2,3},{4,5},{5,6},{6,7},{8,9},{9,10},{10,11},{12,13},{... | collective-permute-start | bytes 49160 | tf_op jit(solution)/shard_map/ppermute | solution.py:15
  119.6 6.4 %collective-permute-start.29 = (f32[4,1,1024]{2,1,0:T(1,128)S(1)}, f32[4,1,1024]{2,1,0:T(1,128)S(1)}, u32[]{:S(2)}, u32[]{:S(2)}) collective-permute-start(f32[4,1,1024]{2,1,0:T(1,128)S(1)} %get-tuple-element.43), channel_id=1, source_target_pairs={{1,0},{2,1},{3,2},{5,4},{6,5},{7,6},{9,8},{10,9},{11,10},{13,12},{... | collective-permute-start | bytes 49160 | tf_op jit(solution)/shard_map/ppermute | solution.py:18
  120.9 5.7 %collective-permute-start.28 = (f32[4,1,1024]{2,1,0:T(1,128)S(1)}, f32[4,1,1024]{2,1,0:T(1,128)S(1)}, u32[]{:S(2)}, u32[]{:S(2)}) collective-permute-start(f32[4,1,1024]{2,1,0:T(1,128)S(1)} %get-tuple-element.42), channel_id=1, source_target_pairs={{0,1},{1,2},{2,3},{4,5},{5,6},{6,7},{8,9},{9,10},{10,11},{12,13},{... | collective-permute-start | bytes 49160 | tf_op jit(solution)/shard_map/ppermute | solution.py:15
  127.0 6.4 %collective-permute-start.31 = (f32[4,1,1024]{2,1,0:T(1,128)S(1)}, f32[4,1,1024]{2,1,0:T(1,128)S(1)}, u32[]{:S(2)}, u32[]{:S(2)}) collective-permute-start(f32[4,1,1024]{2,1,0:T(1,128)S(1)} %get-tuple-element.41), channel_id=1, source_target_pairs={{1,0},{2,1},{3,2},{5,4},{6,5},{7,6},{9,8},{10,9},{11,10},{13,12},{... | collective-permute-start | bytes 49160 | tf_op jit(solution)/shard_map/ppermute | solution.py:18
  128.3 5.7 %collective-permute-start.30 = (f32[4,1,1024]{2,1,0:T(1,128)S(1)}, f32[4,1,1024]{2,1,0:T(1,128)S(1)}, u32[]{:S(2)}, u32[]{:S(2)}) collective-permute-start(f32[4,1,1024]{2,1,0:T(1,128)S(1)} %get-tuple-element.40), channel_id=1, source_target_pairs={{0,1},{1,2},{2,3},{4,5},{5,6},{6,7},{8,9},{9,10},{10,11},{12,13},{... | collective-permute-start | bytes 49160 | tf_op jit(solution)/shard_map/ppermute | solution.py:15
  134.3 6.4 %collective-permute-start.33 = (f32[4,1,1024]{2,1,0:T(1,128)S(1)}, f32[4,1,1024]{2,1,0:T(1,128)S(1)}, u32[]{:S(2)}, u32[]{:S(2)}) collective-permute-start(f32[4,1,1024]{2,1,0:T(1,128)S(1)} %get-tuple-element.39), channel_id=1, source_target_pairs={{1,0},{2,1},{3,2},{5,4},{6,5},{7,6},{9,8},{10,9},{11,10},{13,12},{... | collective-permute-start | bytes 49160 | tf_op jit(solution)/shard_map/ppermute | solution.py:18
  135.6 5.7 %collective-permute-start.32 = (f32[4,1,1024]{2,1,0:T(1,128)S(1)}, f32[4,1,1024]{2,1,0:T(1,128)S(1)}, u32[]{:S(2)}, u32[]{:S(2)}) collective-permute-start(f32[4,1,1024]{2,1,0:T(1,128)S(1)} %get-tuple-element.38), channel_id=1, source_target_pairs={{0,1},{1,2},{2,3},{4,5},{5,6},{6,7},{8,9},{9,10},{10,11},{12,13},{... | collective-permute-start | bytes 49160 | tf_op jit(solution)/shard_map/ppermute | solution.py:15
  141.6 6.4 %collective-permute-start.35 = (f32[4,1,1024]{2,1,0:T(1,128)S(1)}, f32[4,1,1024]{2,1,0:T(1,128)S(1)}, u32[]{:S(2)}, u32[]{:S(2)}) collective-permute-start(f32[4,1,1024]{2,1,0:T(1,128)S(1)} %get-tuple-element.37), channel_id=1, source_target_pairs={{1,0},{2,1},{3,2},{5,4},{6,5},{7,6},{9,8},{10,9},{11,10},{13,12},{... | collective-permute-start | bytes 49160 | tf_op jit(solution)/shard_map/ppermute | solution.py:18
  142.9 5.7 %collective-permute-start.34 = (f32[4,1,1024]{2,1,0:T(1,128)S(1)}, f32[4,1,1024]{2,1,0:T(1,128)S(1)}, u32[]{:S(2)}, u32[]{:S(2)}) collective-permute-start(f32[4,1,1024]{2,1,0:T(1,128)S(1)} %get-tuple-element.36), channel_id=1, source_target_pairs={{0,1},{1,2},{2,3},{4,5},{5,6},{6,7},{8,9},{9,10},{10,11},{12,13},{... | collective-permute-start | bytes 49160 | tf_op jit(solution)/shard_map/ppermute | solution.py:15
  150.5 16.6 %all-to-all-start = ((f32[1,8,8192]{2,0,1:T(1,128)}), f32[1,8,8192]{2,0,1:T(1,128)S(1)}, u32[]{:S(2)}, u32[]{:S(2)}) async-start(f32[1,8,8192]{2,0,1:T(1,128)} %all_to_all.27), calls=%async_computation | async-start | bytes 524288 | tf_op jit(solution)/shard_map/all_to_all | solution.py:126
  185.9 50.6 %all-to-all-start.1 = ((f32[8,1,8192]{2,1,0:T(1,128)}), f32[8,1,8192]{2,1,0:T(1,128)S(1)}, u32[]{:S(2)}, u32[]{:S(2)}) async-start(f32[8,1,8192]{2,1,0:T(1,128)} %copy.67), calls=%async_computation.1 | async-start | bytes 524288 | tf_op jit(solution)/shard_map/all_to_all | solution.py:139
  (11 other events, 50.9 us)
where the time goes:
time: 241 us; the launch traced here: 239 us
  starting transfers between devices  112 us (46%)
  blocking collectives  43.9 us (18%)
  local copies, waits for them, and re-layouts  37.5 us (16%)
  waiting for transfers between devices  18.6 us (8%)
  matrix products  13.5 us (6%)
  other arithmetic  8.53 us (4%)
  between operations  4.62 us (2%)
    ppermute x17, starting transfers between devices, padded_2(): lax.ppermute(lax.slice_in_dim(block, block.shape[dim] - width, None, axis...  73.3 us
    psum x1, blocking collectives, on_device(): square_sum = lax.psum(jnp.sum(gradient * gradient), ('tm', 'space'))  43.9 us
    ppermute x17, starting transfers between devices, padded_2(): lax.ppermute(lax.slice_in_dim(block, 0, width, axis=dim), axis, backward)  22.1 us
    slice x17, local copies, waits for them, and re-layouts, on_device(): lax.associative_scan(combine, (next_cols, inno_cols * forward_cols), reve...  16.4 us
    ppermute x2, waiting for transfers between devices, passed_along(): lax.ppermute(value, axis, [(source, source + steps) for source in range(l...  11.7 us
    dot_general x8, matrix products, select_rows(): jnp.einsum('kb,cbrx->kcrx', picker, blocks, precision=lax.Precision.HIGHEST)  7.44 us
    slice x11, local copies, waits for them, and re-layouts, on_device(): lax.associative_scan(combine, (rate_cols, inno_cols * columns), axis=0)[1]  7.18 us
    all_to_all x1, starting transfers between devices, on_device(): lax.all_to_all(flat_grad, 'tm', split_axis=1, concat_axis=0, tiled=True)  6.3 us
  transfers between devices with their start and end apart: 38, of which 16 were waited for; matrix products, arithmetic and copies ran while one was open for 13% of the time, Pallas kernels for 0%

commit v1 on v0

v1 whole, which is shorter than its diff:
```python
import functools

import jax
import jax.numpy as jnp
from jax import lax
from jax.experimental import pallas as pl
from jax.experimental.pallas import tpu as pltpu
from jax.sharding import PartitionSpec as P

MESH = pl.DeviceIdType.MESH
LANES = 128


def kernel(
    tm,
    space,
    rows_smem,
    weight_smem,
    einv_smem,
    rates_smem,
    ck_hbm,
    adv_hbm,
    dif_hbm,
    obs_hbm,
    back_ref,
    sums_ref,
    states,
    adv,
    dif,
    coef,
    obs,
    pull,
    count,
    next_ck,
    next_einv,
    prior_end,
    costate,
    grads,
    gathered,
    scanned,
    part,
    part_tm,
    part_space,
    local_sem,
    halo_send,
    halo_recv,
    pull_send,
    pull_recv,
    edge_send,
    edge_recv,
    a2a_send,
    a2a_recv,
    ret_send,
    ret_recv,
    sum_send,
    sum_recv,
):
    comps, rows, cols = ck_hbm.shape
    steps, kobs, _, block, _ = obs_hbm.shape
    halo = 2 * steps
    wide = rows + 2 * halo
    share = grads.shape[1]
    tiles = rows // block
    me = lax.axis_index("tm")
    sp = lax.axis_index("space")
    own = pl.ds(halo, rows)
    copies = []

    def send(src, dst, ssem, rsem, target, guard=None):
        copy = pltpu.make_async_remote_copy(
            src_ref=src, dst_ref=dst, send_sem=ssem, recv_sem=rsem,
            device_id=target, device_id_type=MESH,
        )
        if guard is None:
            copy.start()
        else:
            pl.when(guard)(copy.start)
        copies.append((copy, guard))
        return copy

    def landed(copy, guard=None):
        if guard is None:
            copy.wait_recv()
        else:
            pl.when(guard)(copy.wait_recv)

    has_north = sp < space - 1
    has_south = sp > 0
    north = {"space": jnp.minimum(sp + 1, space - 1)}
    south = {"space": jnp.maximum(sp - 1, 0)}
    has_next = me < tm - 1
    has_prev = me > 0
    nxt = {"tm": jnp.minimum(me + 1, tm - 1)}
    prv = {"tm": jnp.maximum(me - 1, 0)}

    loads = [
        pltpu.make_async_copy(dif_hbm, dif.at[own], local_sem.at[0]),
        pltpu.make_async_copy(adv_hbm, adv.at[:, own], local_sem.at[1]),
        pltpu.make_async_copy(ck_hbm, states.at[0, :, own], local_sem.at[2]),
        pltpu.make_async_copy(obs_hbm, obs, local_sem.at[3]),
    ]
    for load in loads:
        load.start()

    barrier = pltpu.get_barrier_semaphore()
    for o in range(1, tm):
        pl.semaphore_signal(
            barrier, inc=1, device_id={"tm": lax.rem(me + o, tm)}, device_id_type=MESH
        )
    for o in range(1, space):
        pl.semaphore_signal(
            barrier, inc=1, device_id={"space": lax.rem(sp + o, space)}, device_id_type=MESH
        )

    weight = weight_smem[0]
    low_halo = pl.ds(0, halo)
    high_halo = pl.ds(halo + rows, halo)

    @pl.when(jnp.logical_not(has_south))
    def _():
        states[0, :, 0:halo, :] = jnp.zeros((comps, halo, cols), jnp.float32)
        adv[:, 0:halo, :] = jnp.zeros((2, halo, cols), jnp.float32)
        dif[0:halo, :] = jnp.zeros((halo, cols), jnp.float32)
        pull[:, :, 0:block, :] = jnp.zeros((steps, comps, block, cols), jnp.float32)
        count[:, 0] = jnp.zeros((steps, block, LANES), jnp.float32)

    @pl.when(jnp.logical_not(has_north))
    def _():
        states[0, :, halo + rows : wide, :] = jnp.zeros((comps, halo, cols), jnp.float32)
        adv[:, halo + rows : wide, :] = jnp.zeros((2, halo, cols), jnp.float32)
        dif[halo + rows : wide, :] = jnp.zeros((halo, cols), jnp.float32)
        pull[:, :, block + rows :, :] = jnp.zeros((steps, comps, block, cols), jnp.float32)
        count[:, tiles + 1] = jnp.zeros((steps, block, LANES), jnp.float32)

    @pl.when(jnp.logical_not(has_next))
    def _():
        next_ck[...] = jnp.zeros_like(next_ck)
        next_einv[...] = jnp.zeros_like(next_einv)

    @pl.when(jnp.logical_not(has_prev))
    def _():
        prior_end[...] = jnp.zeros_like(prior_end)

    for c in range(comps):
        part[1, c : c + 1, :] = jnp.full((1, LANES), einv_smem[0, c], jnp.float32)

    @pl.loop(0, steps)
    def _(t):
        for b in range(tiles):
            total = jnp.float32(0.0)
            for i in range(kobs):
                total = total + jnp.where(rows_smem[t, i] == b, weight, 0.0)
            count[t, b + 1] = jnp.full((block, LANES), total, jnp.float32)

    for load in loads[:3]:
        load.wait()
    pl.semaphore_wait(barrier, tm + space - 2)

    halos = []
    for k, (ref, sem) in enumerate(((dif, 0), (adv, 1), (states.at[0], 2))):
        lead = (slice(None),) * (len(ref.shape) - 2)
        source = ref.at[lead + (own,)]
        halos.append(
            (
                send(source, ref.at[lead + (low_halo,)], halo_send.at[0, k], halo_recv.at[0, k], north, has_north),
                send(source, ref.at[lead + (high_halo,)], halo_send.at[1, k], halo_recv.at[1, k], south, has_south),
            )
        )
    ck_copy = send(states.at[0, :, own], next_ck, edge_send.at[0], edge_recv.at[0], prv, has_prev)
    einv_copy = send(part.at[1], next_einv, edge_send.at[1], edge_recv.at[1], prv, has_prev)
    count_copies = (
        send(count.at[:, tiles], count.at[:, 0], halo_send.at[0, 3], halo_recv.at[0, 3], north, has_north),
        send(count.at[:, 1], count.at[:, tiles + 1], halo_send.at[1, 3], halo_recv.at[1, 3], south, has_south),
    )

    loads[3].wait()

    @pl.loop(0, steps)
    def _(t):
        for b in range(tiles):
            picks = [jnp.where(rows_smem[t, i] == b, weight, 0.0) for i in range(kobs)]
            for c in range(comps):
                total = picks[0] * obs[t, 0, c]
                for i in range(1, kobs):
                    total = total + picks[i] * obs[t, i, c]
                pull[t, c, block * (b + 1) : block * (b + 2), :] = total

    pull_copies = {}

    def send_pull(t):
        pull_copies[t] = (
            send(
                pull.at[t, :, pl.ds(rows, block)], pull.at[t, :, pl.ds(0, block)],
                pull_send.at[0, t], pull_recv.at[0, t], north, has_north,
            ),
            send(
                pull.at[t, :, pl.ds(block, block)], pull.at[t, :, pl.ds(block + rows, block)],
                pull_send.at[1, t], pull_recv.at[1, t], south, has_south,
            ),
        )

    for t in range(steps - 2, -1, -1):
        send_pull(t)

    def both_landed(pair):
        landed(pair[0], has_south)
        landed(pair[1], has_north)

    both_landed(halos[0])
    both_landed(halos[1])
    for r in range(0, wide, 8):
        at = slice(r, r + 8)
        d, a0, a1 = dif[at], adv[0, at], adv[1, at]
        coef[0, at] = 1.0 - 4.0 * d
        coef[1, at] = d - 0.5 * a0
        coef[2, at] = d + 0.5 * a0
        coef[3, at] = d - 0.5 * a1
        coef[4, at] = d + 0.5 * a1
    both_landed(halos[2])

    def forward(c):
        @pl.loop(0, steps)
        def _(t):
            v = states[t, c]
            states[t + 1, c] = (
                coef[0] * v
                + coef[1] * pltpu.roll(v, cols - 1, 1)
                + coef[2] * pltpu.roll(v, 1, 1)
                + coef[3] * pltpu.roll(v, wide - 1, 0)
                + coef[4] * pltpu.roll(v, 1, 0)
            )

    half = comps // 2

    @pl.loop(0, half)
    def _(c):
        forward(c)

    landed(ck_copy, has_next)
    landed(einv_copy, has_next)

    @pl.loop(0, comps)
    def _(c):
        scale = jnp.concatenate([next_einv[pl.ds(c, 1), :]] * (cols // LANES), axis=1)
        inner = pl.ds(block, rows)
        pull[steps - 1, c, inner] = pull[steps - 1, c, inner] + scale * next_ck[c]

    send_pull(steps - 1)

    @pl.loop(half, comps)
    def _(c):
        forward(c)

    end_copy = send(
        states.at[steps, :, own], prior_end, edge_send.at[2], edge_recv.at[2], nxt, has_next
    )

    both_landed(count_copies)
    for t in range(steps - 1, -1, -1):
        both_landed(pull_copies[t])

    inner_rows = rows + 2 * block
    first = halo - block
    inner = pl.ds(first, inner_rows)

    def adjoint(c):
        scale = jnp.concatenate([next_einv[pl.ds(c, 1), :]] * (cols // LANES), axis=1)

        def force(t):
            marks = [
                jnp.concatenate([count[t, q]] * (cols // LANES), axis=1) for q in range(tiles + 2)
            ]
            return jnp.concatenate(marks, axis=0) * states[t + 1, c, inner] - pull[t, c]

        costate[...] = force(steps - 1) + scale * states[steps, c, inner]

        def step(w):
            return (
                coef[0, inner] * w
                + pltpu.roll(coef[1, inner] * w, 1, 1)
                + pltpu.roll(coef[2, inner] * w, cols - 1, 1)
                + pltpu.roll(coef[3, inner] * w, 1, 0)
                + pltpu.roll(coef[4, inner] * w, inner_rows - 1, 0)
            )

        @pl.loop(0, steps - 1)
        def _(s):
            costate[...] = step(costate[...]) + force(steps - 2 - s)

        last = step(costate[...])[block : block + rows]
        states[0, c, 0:rows, :] = last

    @pl.loop(0, comps)
    def _(c):
        adjoint(c)

    landed(end_copy, has_prev)

    per = rows // share
    squares = jnp.zeros((8, LANES), jnp.float32)
    for c in range(comps):
        scale = einv_smem[0, c]
        g = states[0, c, 0:rows, :] + scale * (states[0, c, own] - prior_end[c])
        for h in range(per):
            grads[c * per + h] = g[h * share : (h + 1) * share]
        sq = g * g
        for r in range(0, rows, 8):
            for l in range(0, cols, LANES):
                squares = squares + sq[r : r + 8, l : l + LANES]
    part[0] = squares

    gather = []
    sums = []
    for o in range(1, tm):
        peer = lax.rem(me + o, tm)
        gather.append(
            send(grads.at[peer], gathered.at[me], a2a_send.at[o], a2a_recv.at[o], {"tm": peer})
        )
    for o in range(1, tm):
        peer = lax.rem(me + o, tm)
        sums.append(
            send(part.at[0], part_tm.at[me], sum_send.at[o], sum_recv.at[o], {"tm": peer})
        )
    part_tm[me] = squares
    gathered[me] = grads[me]
    for copy in gather:
        copy.wait_recv()

    k = me * share // rows

    def rate(j):
        return jnp.full((1, cols), rates_smem[j, k], jnp.float32)

    running = jnp.zeros((share, cols), jnp.float32)
    for j in range(tm):
        r = rate(j)
        running = r * running + jnp.sqrt(1.0 - r * r) * gathered[j]
        scanned[j] = running
    running = jnp.zeros((share, cols), jnp.float32)
    for j in range(tm - 1, -1, -1):
        r = rate(j)
        running = jnp.sqrt(1.0 - r * r) * scanned[j] + running
        scanned[j] = running
        running = r * running

    returns = []
    for o in range(1, tm):
        peer = lax.rem(me + o, tm)
        returns.append(
            send(scanned.at[peer], back_ref.at[me], ret_send.at[o], ret_recv.at[o], {"tm": peer})
        )
    back_ref[me] = scanned[me]

    for copy in sums:
        copy.wait_recv()
    total = part_tm[0]
    for j in range(1, tm):
        total = total + part_tm[j]
    part_space[sp] = total
    part[2] = total
    across = []
    for o in range(1, space):
        peer = lax.rem(sp + o, space)
        across.append(
            send(part.at[2], part_space.at[sp], sum_send.at[tm + o], sum_recv.at[tm + o], {"space": peer})
        )
    for copy in across:
        copy.wait_recv()
    total = part_space[0]
    for j in range(1, space):
        total = total + part_space[j]
    sums_ref[...] = total
    for copy in returns:
        copy.wait_recv()
    for copy, guard in copies:
        if guard is None:
            copy.wait_send()
        else:
            pl.when(guard)(copy.wait_send)


def on_device(tm, space, checkpoint, advect, diffuse, obs_rows, obs_values, obs_weight, error_inverse, rates):
    comps, rows, cols = checkpoint.shape[1:]
    steps, kobs, _, block, _ = obs_values.shape[1:]
    halo = 2 * steps
    wide = rows + 2 * halo
    tiles = rows // block
    share = comps * rows // tm
    f32 = jnp.float32
    smem = pl.BlockSpec(memory_space=pltpu.SMEM)
    hbm = pl.BlockSpec(memory_space=pl.ANY)
    vmem = pl.BlockSpec(memory_space=pltpu.VMEM)
    dma = pltpu.SemaphoreType.DMA
    back, sums = pl.pallas_call(
        functools.partial(kernel, tm, space),
        out_shape=(
            jax.ShapeDtypeStruct((tm, share, cols), f32),
            jax.ShapeDtypeStruct((8, LANES), f32),
        ),
        in_specs=[smem] * 4 + [hbm] * 4,
        out_specs=(vmem, vmem),
        scratch_shapes=[
            pltpu.VMEM((steps + 1, comps, wide, cols), f32),
            pltpu.VMEM((2, wide, cols), f32),
            pltpu.VMEM((wide, cols), f32),
            pltpu.VMEM((5, wide, cols), f32),
            pltpu.VMEM((steps, kobs, comps, block, cols), f32),
            pltpu.VMEM((steps, comps, rows + 2 * block, cols), f32),
            pltpu.VMEM((steps, tiles + 2, block, LANES), f32),
            pltpu.VMEM((comps, rows, cols), f32),
            pltpu.VMEM((8, LANES), f32),
            pltpu.VMEM((comps, rows, cols), f32),
            pltpu.VMEM((rows + 2 * block, cols), f32),
            pltpu.VMEM((tm, share, cols), f32),
            pltpu.VMEM((tm, share, cols), f32),
            pltpu.VMEM((tm, share, cols), f32),
            pltpu.VMEM((3, 8, LANES), f32),
            pltpu.VMEM((tm, 8, LANES), f32),
            pltpu.VMEM((space, 8, LANES), f32),
            dma((4,)),
            dma((2, 4)),
            dma((2, 4)),
            dma((2, steps)),
            dma((2, steps)),
            dma((3,)),
            dma((3,)),
            dma((tm,)),
            dma((tm,)),
            dma((tm,)),
            dma((tm,)),
            dma((tm + space,)),
            dma((tm + space,)),
        ],
        compiler_params=pltpu.CompilerParams(
            collective_id=0, has_side_effects=True, vmem_limit_bytes=48 * 1024 * 1024
        ),
    )(
        obs_rows[0], obs_weight, error_inverse, rates,
        checkpoint[0], advect[0], diffuse[0], obs_values[0],
    )
    entries = tm * space * checkpoint.size
    rms_value = jnp.sqrt(jnp.sum(sums) / entries + 1e-06)
    direction = back.reshape(checkpoint.shape) / rms_value
    return direction, rms_value


def solution(mesh):
    placed = (
        P("tm", None, "space", None),
        P("tm", None, "space", None),
        P("tm", "space", None),
        P("tm", None, "space"),
        P("tm", None, "space", None, None, None),
        P("tm"),
        P("tm", None),
        P(),
    )
    return jax.shard_map(
        functools.partial(on_device, mesh.shape["tm"], mesh.shape["space"]),
        mesh=mesh,
        in_specs=placed,
        out_specs=(P("tm", None, "space", None), P()),
        check_vma=False,
    )
```

time: 241 us -> 52.7 us (0.22)
  the two profiles are of different devices: /device:TPU:0 before, /device:TPU:1 now
where the time goes in v1:
time: 52.7 us; the launch traced here: 52.4 us
  Pallas kernels  41.5 us (79%)
  local copies, waits for them, and re-layouts  6.45 us (12%)
  between operations  3.12 us (6%)
  other arithmetic  1.33 us (3%)
    pallas_call x1, Pallas kernels, on_device(): pl.pallas_call(functools.partial(kernel, tm, space), out_shape=(jax.Shape...  41.5 us
    unnamed x11, local copies, waits for them, and re-layouts  5.69 us

profile of v1, /device:TPU:1, one launch (start us, length us, event | category | flops | bytes accessed | tf_op | source)
XLA Modules:
  0.0 52.4 jit_solution(11225965950911437114)
XLA Ops:
  1.3 0.8 %copy.10.rows_smem = s32[8,2]{1,0:T(8,128)S(1)} copy(s32[8,2]{0,1:T(2,128)} %bitcast.11) | data formatting | bytes 128 | tf_op jit(solution)/shard_map/squeeze | solution.py:438
  2.0 0.8 %copy.11.rates_smem = f32[8,4]{1,0:T(8,128)S(1)} copy(f32[8,4]{0,1:T(4,128)} %param.15) | data formatting | bytes 256 | tf_op args[7]
  2.8 0.0 copy-start
  2.8 1.6 %copy-done = f32[1,8,2,4,8,1024]{5,4,3,2,1,0:T(8,128)S(1)} copy-done((f32[1,8,2,4,8,1024]{5,4,3,2,1,0:T(8,128)S(1)}, f32[1,8,2,4,8,1024]{5,4,3,2,1,0:T(8,128)}, u32[]{:S(2)}) %copy-start) | copy-done | bytes 2097176
  4.4 0.0 copy-start.1
  4.4 0.9 %copy-done.1 = f32[1,4,16,1024]{3,2,1,0:T(8,128)S(1)} copy-done((f32[1,4,16,1024]{3,2,1,0:T(8,128)S(1)}, f32[1,4,16,1024]{3,2,1,0:T(8,128)}, u32[]{:S(2)}) %copy-start.1) | copy-done | bytes 262168
  5.3 0.0 copy-start.2
  5.3 0.9 %copy-done.2 = f32[1,2,16,1024]{3,2,1,0:T(8,128)S(1)} copy-done((f32[1,2,16,1024]{3,2,1,0:T(8,128)S(1)}, f32[1,2,16,1024]{3,2,1,0:T(8,128)}, u32[]{:S(2)}) %copy-start.2) | copy-done | bytes 131096
  6.2 0.0 copy-start.3
  6.2 0.8 %copy-done.3 = f32[1,16,1024]{2,1,0:T(8,128)S(1)} copy-done((f32[1,16,1024]{2,1,0:T(8,128)S(1)}, f32[1,16,1024]{2,1,0:T(8,128)}, u32[]{:S(2)}) %copy-start.3) | copy-done | bytes 65560
  7.1 0.0 copy-start.4
  7.1 0.7 %copy-done.4 = f32[1,4]{1,0:T(1,128)S(1)} copy-done((f32[1,4]{1,0:T(1,128)S(1)}, f32[1,4]{1,0:T(1,128)}, u32[]{:S(2)}) %copy-start.4) | copy-done | bytes 40
  7.7 41.5 %shard_map.95 = (f32[8,8,1024]{2,1,0:T(8,128)S(1)}, f32[8,128]{1,0:T(8,128)S(1)}) custom-call(s32[8,2]{1,0:T(8,128)S(1)} %copy.10.rows_smem, f32[1]{0:T(128)S(6)} %copy.12.weight_smem, f32[1,4]{1,0:T(1,128)S(1)} %copy-done.4, f32[8,4]{1,0:T(8,128)S(1)} %copy.11.rates_smem, f32[4,16,1024]{2,1,0:T(8,128)S(1)} %bitcast.7, f32[2,16,1024]{2,1,0:T(8,128)S(1)} %bitcast.8, ...), custom_call_target="tpu_custom_call" | custom-call | tf_op jit(solution)/shard_map/pallas_call | solution.py:394
  49.2 0.6 %reduce_sum.9 = f32[]{:T(128)} reduce(f32[8,128]{1,0:T(8,128)S(1)} %get-tuple-element.5, f32[]{:T(128)} %constant.1.clone.1), dimensions={0,1}, to_apply=%region_0.0 | reduce | flops 1023 | bytes 4104 | tf_op jit(solution)/shard_map/reduce_sum | solution.py:442
  50.5 0.7 %broadcast_divide_fusion = f32[8,8,1024]{2,1,0:T(8,128)} fusion(f32[8,8,1024]{2,1,0:T(8,128)S(1)} %get-tuple-element.4, f32[]{:T(128)} %sqrt.3), kind=kLoop, calls=%fused_computation | loop fusion | flops 65536 | bytes 524292 | tf_op jit(solution)/shard_map/div | solution.py:443
Async XLA Ops:
  2.8 1.6 %copy-start = (f32[1,8,2,4,8,1024]{5,4,3,2,1,0:T(8,128)S(1)}, f32[1,8,2,4,8,1024]{5,4,3,2,1,0:T(8,128)}, u32[]{:S(2)}) copy-start(f32[1,8,2,4,8,1024]{5,4,3,2,1,0:T(8,128)} %param.12) | copy-start | bytes 6291460
  4.4 0.9 %copy-start.1 = (f32[1,4,16,1024]{3,2,1,0:T(8,128)S(1)}, f32[1,4,16,1024]{3,2,1,0:T(8,128)}, u32[]{:S(2)}) copy-start(f32[1,4,16,1024]{3,2,1,0:T(8,128)} %param.8) | copy-start | bytes 786436
  5.3 0.9 %copy-start.2 = (f32[1,2,16,1024]{3,2,1,0:T(8,128)S(1)}, f32[1,2,16,1024]{3,2,1,0:T(8,128)}, u32[]{:S(2)}) copy-start(f32[1,2,16,1024]{3,2,1,0:T(8,128)} %param.9) | copy-start | bytes 393220
  6.2 0.8 %copy-start.3 = (f32[1,16,1024]{2,1,0:T(8,128)S(1)}, f32[1,16,1024]{2,1,0:T(8,128)}, u32[]{:S(2)}) copy-start(f32[1,16,1024]{2,1,0:T(8,128)} %param.10) | copy-start | bytes 196612
  7.1 0.7 %copy-start.4 = (f32[1,4]{1,0:T(1,128)S(1)}, f32[1,4]{1,0:T(1,128)}, u32[]{:S(2)}) copy-start(f32[1,4]{1,0:T(1,128)} %einv_smem.1) | copy-start | bytes 52

commit v2 on v1

v2 whole, which is shorter than its diff:
```python
import functools

import jax
import jax.numpy as jnp
from jax import lax
from jax.experimental import pallas as pl
from jax.experimental.pallas import tpu as pltpu
from jax.sharding import PartitionSpec as P

MESH = pl.DeviceIdType.MESH
LANES = 128


def kernel(
    tm,
    space,
    rows_hbm,
    weight_hbm,
    einv_hbm,
    rates_hbm,
    ck_hbm,
    adv_hbm,
    dif_hbm,
    obs_hbm,
    back_ref,
    rms_ref,
    rows_smem,
    weight_smem,
    einv_smem,
    rates_smem,
    states,
    adv,
    dif,
    coef,
    obs,
    pull,
    count,
    next_ck,
    next_einv,
    prior_end,
    costate,
    grads,
    gathered,
    scanned,
    returned,
    part,
    part_tm,
    part_space,
    local_sem,
    halo_send,
    halo_recv,
    ck_send,
    ck_recv,
    pull_send,
    pull_recv,
    edge_send,
    edge_recv,
    end_send,
    end_recv,
    a2a_send,
    a2a_recv,
    ret_send,
    ret_recv,
    sum_send,
    sum_recv,
):
    comps, rows, cols = ck_hbm.shape
    steps, kobs, _, block, _ = obs_hbm.shape
    halo = 2 * steps
    wide = rows + 2 * halo
    tiles = rows // block
    tall, across_cols = grads.shape[2:]
    col_groups = cols // across_cols
    me = lax.axis_index("tm")
    sp = lax.axis_index("space")
    own = pl.ds(halo, rows)
    low_halo = pl.ds(0, halo)
    high_halo = pl.ds(halo + rows, halo)
    copies = []

    def send(src, dst, ssem, rsem, target, guard=None):
        copy = pltpu.make_async_remote_copy(
            src_ref=src, dst_ref=dst, send_sem=ssem, recv_sem=rsem,
            device_id=target, device_id_type=MESH,
        )
        if guard is None:
            copy.start()
        else:
            pl.when(guard)(copy.start)
        copies.append((copy, guard))
        return copy

    def landed(copy, guard=None):
        if guard is None:
            copy.wait_recv()
        else:
            pl.when(guard)(copy.wait_recv)

    has_north = sp < space - 1
    has_south = sp > 0
    north = {"space": jnp.minimum(sp + 1, space - 1)}
    south = {"space": jnp.maximum(sp - 1, 0)}
    has_next = me < tm - 1
    has_prev = me > 0
    nxt = {"tm": jnp.minimum(me + 1, tm - 1)}
    prv = {"tm": jnp.maximum(me - 1, 0)}

    barrier = pltpu.get_barrier_semaphore()
    for o in range(1, tm):
        pl.semaphore_signal(
            barrier, inc=1, device_id={"tm": lax.rem(me + o, tm)}, device_id_type=MESH
        )
    for o in range(1, space):
        pl.semaphore_signal(
            barrier, inc=1, device_id={"space": lax.rem(sp + o, space)}, device_id_type=MESH
        )

    loads = [
        pltpu.make_async_copy(source, target, local_sem.at[k])
        for k, (source, target) in enumerate(
            (
                (dif_hbm, dif.at[own]),
                (adv_hbm, adv.at[:, own]),
                (ck_hbm, states.at[0, :, own]),
                (rows_hbm, rows_smem),
                (weight_hbm, weight_smem),
                (einv_hbm, einv_smem),
                (rates_hbm, rates_smem),
                (obs_hbm, obs),
            )
        )
    ]
    for load in loads:
        load.start()

    @pl.when(jnp.logical_not(has_south))
    def _():
        states[0, :, 0:halo, :] = jnp.zeros((comps, halo, cols), jnp.float32)
        adv[:, 0:halo, :] = jnp.zeros((2, halo, cols), jnp.float32)
        dif[0:halo, :] = jnp.zeros((halo, cols), jnp.float32)
        pull[:, :, 0:block, :] = jnp.zeros((comps, steps, block, cols), jnp.float32)
        count[:, 0] = jnp.zeros((steps, block, LANES), jnp.float32)

    @pl.when(jnp.logical_not(has_north))
    def _():
        states[0, :, halo + rows : wide, :] = jnp.zeros((comps, halo, cols), jnp.float32)
        adv[:, halo + rows : wide, :] = jnp.zeros((2, halo, cols), jnp.float32)
        dif[halo + rows : wide, :] = jnp.zeros((halo, cols), jnp.float32)
        pull[:, :, block + rows :, :] = jnp.zeros((comps, steps, block, cols), jnp.float32)
        count[:, tiles + 1] = jnp.zeros((steps, block, LANES), jnp.float32)

    @pl.when(jnp.logical_not(has_next))
    def _():
        next_ck[...] = jnp.zeros_like(next_ck)
        next_einv[...] = jnp.zeros_like(next_einv)

    @pl.when(jnp.logical_not(has_prev))
    def _():
        prior_end[...] = jnp.zeros_like(prior_end)

    middle = steps // 2
    near = min(middle, block)
    if near < block:
        blank = jnp.zeros((comps, middle, block - near, cols), jnp.float32)
        pull[:, 0:middle, 0 : block - near, :] = blank
        pull[:, 0:middle, block + rows + near :, :] = blank

    for load in loads[:3]:
        load.wait()
    pl.semaphore_wait(barrier, tm + space - 2)

    def both_ways(ref, ssem, rsem):
        lead = (slice(None),) * (len(ref.shape) - 2)
        source = ref.at[lead + (own,)]
        return (
            send(source, ref.at[lead + (low_halo,)], ssem.at[0], rsem.at[0], north, has_north),
            send(source, ref.at[lead + (high_halo,)], ssem.at[1], rsem.at[1], south, has_south),
        )

    def both_landed(pair):
        landed(pair[0], has_south)
        landed(pair[1], has_north)

    def send_ck_halo(c):
        return both_ways(states.at[0, c], ck_send.at[c], ck_recv.at[c])

    halos = [
        both_ways(dif, halo_send.at[0], halo_recv.at[0]),
        both_ways(adv, halo_send.at[1], halo_recv.at[1]),
    ]
    ck_halos = [send_ck_halo(0)]
    next_copies = [
        send(states.at[0, c, own], next_ck.at[c], edge_send.at[c], edge_recv.at[c], prv, has_prev)
        for c in range(comps)
    ]

    for load in loads[3:7]:
        load.wait()
    weight = weight_smem[0]
    for c in range(comps):
        part[1, c : c + 1, :] = jnp.full((1, LANES), einv_smem[0, c], jnp.float32)

    @pl.loop(0, steps)
    def _(t):
        for b in range(tiles):
            total = jnp.float32(0.0)
            for i in range(kobs):
                total = total + jnp.where(rows_smem[i, t] == b, weight, 0.0)
            count[t, b + 1] = jnp.full((block, LANES), total, jnp.float32)

    einv_copy = send(part.at[1], next_einv, edge_send.at[comps], edge_recv.at[comps], prv, has_prev)
    count_copies = (
        send(count.at[:, tiles], count.at[:, 0], halo_send.at[2, 0], halo_recv.at[2, 0], north, has_north),
        send(count.at[:, 1], count.at[:, tiles + 1], halo_send.at[2, 1], halo_recv.at[2, 1], south, has_south),
    )
    loads[7].wait()

    @pl.loop(0, steps)
    def _(t):
        for b in range(tiles):
            picks = [jnp.where(rows_smem[i, t] == b, weight, 0.0) for i in range(kobs)]
            for c in range(comps):
                total = picks[0] * obs[t, 0, c]
                for i in range(1, kobs):
                    total = total + picks[i] * obs[t, i, c]
                pull[c, t, block * (b + 1) : block * (b + 2), :] = total

    spans = ((middle, steps - 1, block), (0, middle, near), (steps - 1, steps, block))

    def send_pull(c, which):
        first, last, depth = spans[which]
        at = pl.ds(first, last - first)
        return (
            send(
                pull.at[c, at, pl.ds(block + rows - depth, depth)],
                pull.at[c, at, pl.ds(block - depth, depth)],
                pull_send.at[c, which, 0], pull_recv.at[c, which, 0], north, has_north,
            ),
            send(
                pull.at[c, at, pl.ds(block, depth)],
                pull.at[c, at, pl.ds(block + rows, depth)],
                pull_send.at[c, which, 1], pull_recv.at[c, which, 1], south, has_south,
            ),
        )

    pulls = {}

    def send_pulls(c):
        pulls[c] = [send_pull(c, 0), send_pull(c, 1)]

    def next_row(c):
        return jnp.concatenate([next_einv[c : c + 1, :]] * (cols // LANES), axis=1)

    def send_last_pull(c):
        landed(next_copies[c], has_next)
        if c == 0:
            landed(einv_copy, has_next)
        inside = slice(block, block + rows)
        pull[c, steps - 1, inside, :] = pull[c, steps - 1, inside, :] + next_row(c) * next_ck[c]
        pulls[c].append(send_pull(c, 2))

    send_pulls(0)
    ck_halos.append(send_ck_halo(1))
    send_pulls(1)

    both_landed(halos[0])
    both_landed(halos[1])
    for r in range(0, wide, 8):
        at = slice(r, r + 8)
        d, a0, a1 = dif[at], adv[0, at], adv[1, at]
        coef[0, at] = 1.0 - 4.0 * d
        coef[1, at] = d - 0.5 * a0
        coef[2, at] = d + 0.5 * a0
        coef[3, at] = d - 0.5 * a1
        coef[4, at] = d + 0.5 * a1
    send_last_pull(0)

    end_copies = {}

    def forward(c):
        both_landed(ck_halos[c])

        @pl.loop(0, steps)
        def _(t):
            v = states[t, c]
            states[t + 1, c] = (
                coef[0] * v
                + coef[1] * pltpu.roll(v, cols - 1, 1)
                + coef[2] * pltpu.roll(v, 1, 1)
                + coef[3] * pltpu.roll(v, wide - 1, 0)
                + coef[4] * pltpu.roll(v, 1, 0)
            )

        end_copies[c] = send(
            states.at[steps, c, own], prior_end.at[c], end_send.at[c], end_recv.at[c], nxt, has_next
        )

    inner_rows = rows + 2 * block
    first = halo - block
    inner = pl.ds(first, inner_rows)
    gather = {}

    def adjoint(c, squares):
        for pair in pulls[c]:
            both_landed(pair)

        def force(t):
            marks = [
                jnp.concatenate([count[t, q]] * (cols // LANES), axis=1) for q in range(tiles + 2)
            ]
            return jnp.concatenate(marks, axis=0) * states[t + 1, c, inner] - pull[c, t]

        costate[...] = force(steps - 1) + next_row(c) * states[steps, c, inner]

        def step(w):
            return (
                coef[0, inner] * w
                + pltpu.roll(coef[1, inner] * w, 1, 1)
                + pltpu.roll(coef[2, inner] * w, cols - 1, 1)
                + pltpu.roll(coef[3, inner] * w, 1, 0)
                + pltpu.roll(coef[4, inner] * w, inner_rows - 1, 0)
            )

        @pl.loop(0, steps - 1)
        def _(s):
            costate[...] = step(costate[...]) + force(steps - 2 - s)

        landed(end_copies[c], has_prev)
        g = step(costate[...])[block : block + rows] + einv_smem[0, c] * (
            states[0, c, own] - prior_end[c]
        )
        for d in range(tm):
            r0, c0 = d // col_groups * tall, d % col_groups * across_cols
            grads[c, d] = g[r0 : r0 + tall, c0 : c0 + across_cols]
        gather[c] = [
            send(
                grads.at[c, lax.rem(me + o, tm)], gathered.at[c, me],
                a2a_send.at[c, o], a2a_recv.at[c, o], {"tm": lax.rem(me + o, tm)},
            )
            for o in range(1, tm)
        ]
        gathered[c, me] = grads[c, me]
        sq = g * g
        for r in range(0, rows, 8):
            for l in range(0, cols, LANES):
                squares = squares + sq[r : r + 8, l : l + LANES]
        return squares

    returns = {}

    def scan(c):
        for copy in gather[c]:
            copy.wait_recv()
        keep = [jnp.full((1, across_cols), rates_smem[c, j], jnp.float32) for j in range(tm)]
        gain = [jnp.sqrt(1.0 - r * r) for r in keep]
        running = jnp.zeros((tall, across_cols), jnp.float32)
        ahead = []
        for j in range(tm):
            running = keep[j] * running + gain[j] * gathered[c, j]
            ahead.append(running)
        running = jnp.zeros((tall, across_cols), jnp.float32)
        for j in range(tm - 1, -1, -1):
            running = gain[j] * ahead[j] + running
            scanned[c, j] = running
            running = keep[j] * running
        returns[c] = [
            send(
                scanned.at[c, lax.rem(me + o, tm)], returned.at[c, me],
                ret_send.at[c, o], ret_recv.at[c, o], {"tm": lax.rem(me + o, tm)},
            )
            for o in range(1, tm)
        ]
        returned[c, me] = scanned[c, me]

    squares = jnp.zeros((8, LANES), jnp.float32)
    forward(0)
    send_last_pull(1)
    ck_halos.append(send_ck_halo(2))
    send_pulls(2)
    forward(1)
    send_last_pull(2)
    ck_halos.append(send_ck_halo(3))
    send_pulls(3)
    both_landed(count_copies)
    squares = adjoint(0, squares)
    send_last_pull(3)
    forward(2)
    forward(3)
    squares = adjoint(1, squares)
    scan(0)
    squares = adjoint(2, squares)
    scan(1)
    squares = adjoint(3, squares)

    part[0] = squares
    sums = [
        send(
            part.at[0], part_tm.at[me], sum_send.at[o], sum_recv.at[o], {"tm": lax.rem(me + o, tm)}
        )
        for o in range(1, tm)
    ]
    part_tm[me] = squares
    scan(2)
    scan(3)

    for copy in sums:
        copy.wait_recv()
    total = part_tm[0]
    for j in range(1, tm):
        total = total + part_tm[j]
    part_space[sp] = total
    part[2] = total
    across = [
        send(
            part.at[2], part_space.at[sp], sum_send.at[tm + o], sum_recv.at[tm + o],
            {"space": lax.rem(sp + o, space)},
        )
        for o in range(1, space)
    ]

    def place(c):
        for copy in returns[c]:
            copy.wait_recv()
        for d in range(tm):
            r0, c0 = d // col_groups * tall, d % col_groups * across_cols
            back_ref[c, r0 : r0 + tall, c0 : c0 + across_cols] = returned[c, d]

    for c in range(comps - 1):
        place(c)
    for copy in across:
        copy.wait_recv()
    total = part_space[0]
    for j in range(1, space):
        total = total + part_space[j]
    entries = tm * space * comps * rows * cols
    rms_ref[...] = jnp.sqrt(jnp.sum(total, axis=(0, 1), keepdims=True) / entries + 1e-06)
    place(comps - 1)
    for copy, guard in copies:
        if guard is None:
            copy.wait_send()
        else:
            pl.when(guard)(copy.wait_send)


def on_device(tm, space, checkpoint, advect, diffuse, obs_rows, obs_values, obs_weight, error_inverse, rates):
    comps, rows, cols = checkpoint.shape[1:]
    steps, kobs, _, block, _ = obs_values.shape[1:]
    halo = 2 * steps
    wide = rows + 2 * halo
    tiles = rows // block
    col_groups = min(tm, cols // LANES)
    chunk = (rows * col_groups // tm, cols // col_groups)
    f32 = jnp.float32
    hbm = pl.BlockSpec(memory_space=pltpu.HBM)
    vmem = pl.BlockSpec(memory_space=pltpu.VMEM)
    dma = pltpu.SemaphoreType.DMA
    back, rms = pl.pallas_call(
        functools.partial(kernel, tm, space),
        out_shape=(
            jax.ShapeDtypeStruct((comps, rows, cols), f32),
            jax.ShapeDtypeStruct((1, 1), f32),
        ),
        in_specs=[hbm] * 8,
        out_specs=(vmem, vmem),
        scratch_shapes=[
            pltpu.SMEM((kobs, steps), jnp.int32),
            pltpu.SMEM((1,), f32),
            pltpu.SMEM((1, comps), f32),
            pltpu.SMEM((comps, tm), f32),
            pltpu.VMEM((steps + 1, comps, wide, cols), f32),
            pltpu.VMEM((2, wide, cols), f32),
            pltpu.VMEM((wide, cols), f32),
            pltpu.VMEM((5, wide, cols), f32),
            pltpu.VMEM((steps, kobs, comps, block, cols), f32),
            pltpu.VMEM((comps, steps, rows + 2 * block, cols), f32),
            pltpu.VMEM((steps, tiles + 2, block, LANES), f32),
            pltpu.VMEM((comps, rows, cols), f32),
            pltpu.VMEM((8, LANES), f32),
            pltpu.VMEM((comps, rows, cols), f32),
            pltpu.VMEM((rows + 2 * block, cols), f32),
            pltpu.VMEM((comps, tm) + chunk, f32),
            pltpu.VMEM((comps, tm) + chunk, f32),
            pltpu.VMEM((comps, tm) + chunk, f32),
            pltpu.VMEM((comps, tm) + chunk, f32),
            pltpu.VMEM((3, 8, LANES), f32),
            pltpu.VMEM((tm, 8, LANES), f32),
            pltpu.VMEM((space, 8, LANES), f32),
            dma((8,)),
            dma((3, 2)),
            dma((3, 2)),
            dma((comps, 2)),
            dma((comps, 2)),
            dma((comps, 3, 2)),
            dma((comps, 3, 2)),
            dma((comps + 1,)),
            dma((comps + 1,)),
            dma((comps,)),
            dma((comps,)),
            dma((comps, tm)),
            dma((comps, tm)),
            dma((comps, tm)),
            dma((comps, tm)),
            dma((tm + space,)),
            dma((tm + space,)),
        ],
        compiler_params=pltpu.CompilerParams(
            collective_id=0, has_side_effects=True, vmem_limit_bytes=60 * 1024 * 1024
        ),
    )(
        obs_rows[0].T, obs_weight, error_inverse, rates.T,
        checkpoint[0], advect[0], diffuse[0], obs_values[0],
    )
    rms_value = rms.reshape(())
    direction = back[None] / rms_value
    return direction, rms_value


def solution(mesh):
    placed = (
        P("tm", None, "space", None),
        P("tm", None, "space", None),
        P("tm", "space", None),
        P("tm", None, "space"),
        P("tm", None, "space", None, None, None),
        P("tm"),
        P("tm", None),
        P(),
    )
    return jax.shard_map(
        functools.partial(on_device, mesh.shape["tm"], mesh.shape["space"]),
        mesh=mesh,
        in_specs=placed,
        out_specs=(P("tm", None, "space", None), P()),
        check_vma=False,
    )
```

time: 52.7 us -> 47.5 us (0.901)
  the two profiles are of different devices: /device:TPU:1 before, /device:TPU:0 now
where the time goes in v2:
time: 47.5 us; the launch traced here: 47.3 us
  Pallas kernels  42 us (88%)
  between operations  3.05 us (6%)
  other arithmetic  2.31 us (5%)
    pallas_call x1, Pallas kernels, on_device(): pl.pallas_call(functools.partial(kernel, tm, space), out_shape=(jax.Shape...  42 us
    div x1, other arithmetic, on_device(): direction = back[None] / rms_value  2.31 us

profile of v2, /device:TPU:0, one launch (start us, length us, event | category | flops | bytes accessed | tf_op | source)
XLA Modules:
  0.0 47.3 jit_solution(11456929663431211312)
XLA Ops:
  1.3 42.0 %shard_map.95 = (f32[4,16,1024]{2,1,0:T(8,128)}, f32[1,1]{1,0:T(1,128)}) custom-call(s32[2,8]{1,0:T(2,128)} %bitcast.16, f32[1]{0:T(128)S(6)} %copy.11.weight_hbm, f32[1,4]{1,0:T(1,128)} %einv_hbm.1, f32[4,8]{1,0:T(4,128)} %bitcast.15, f32[4,16,1024]{2,1,0:T(8,128)} %bitcast.12, f32[2,16,1024]{2,1,0:T(8,128)} %bitcast.13, f32[16,1024]{1,0:T(8,128)} %bitcast.14, ...), custom_call_target="tpu_custom_call" | custom-call | tf_op jit(solution)/shard_map/pallas_call | solution.py:457
  43.3 2.3 %divide_bitcast_fusion = f32[1,4,16,1024]{3,2,1,0:T(8,128)} fusion(f32[4,16,1024]{2,1,0:T(8,128)} %get-tuple-element.4, f32[]{:T(128)} %bitcast.7), kind=kLoop, calls=%fused_computation | loop fusion | flops 65536 | bytes 524292 | tf_op jit(solution)/shard_map/div | solution.py:514
